TPU v7x, 1024 devices: a whole 8x8x8 slice. The times are simulated.
1024 devices in a mesh: rep: 8 (over x_hi, core), dp: 16 (over z, x_lo), tp: 8 (over y).
Axes of the slice: x: 8 (x_hi: 4, x_lo: 2; x = x_hi * 2 + x_lo), y: 8, z: 8, core: 2. Of those that a mesh axis runs over, the one named last changes fastest.
Arguments:
- hidden: bfloat16 [8, 512, 14336], P('rep', None, 'tp'), may hold values from -6 to 6
- down_weight: bfloat16 [14336, 8192], P('tp', 'dp'), may hold values from -0.046875 to 0.046875
- out_grad: bfloat16 [8, 512, 8192], P('rep', 'tp', 'dp'), may hold values from -6 to 6
- pseudo_grad: bfloat16 [8, 14336, 8192], P('rep', 'tp', 'dp'), may hold values from -6 to 6
- momentum: float32 [14336, 8192], P(('tp', 'rep'), 'dp'), may hold values from -6 to 6
Outputs:
- layer_out: bfloat16 [8, 512, 8192], P('rep', 'tp', 'dp')
- hidden_grad: bfloat16 [8, 512, 14336], P('rep', 'dp', 'tp')
- new_momentum: float32 [14336, 8192], P(('tp', 'rep'), 'dp')
- outer_step: bfloat16 [14336, 8192], P('tp', 'dp')
All inputs are finite; a program needn't handle non-finite values.
Results may differ from a plain program's by a relative error of at most 0.017.
Values may be sent and summed in bfloat16 or wider, within the bound.
A program may use at most 64 MiB of HBM per device.

v0:
```python
import jax
import jax.numpy as jnp
from jax import lax
from jax.sharding import PartitionSpec as P

outer_rate = 0.7
momentum_rate = 0.9


def split_up(shard, dim, peers):
    before, after = (shard.shape[:dim], shard.shape[dim + 1 :])
    return jnp.moveaxis(shard.reshape(*before, peers, -1, *after), dim, 0)


def sent_and_summed(shard, axis, dim):
    parts = split_up(shard, dim, lax.axis_size(axis))
    arrived = lax.all_to_all(parts, axis, split_axis=0, concat_axis=0, tiled=True)
    return arrived.astype(jnp.float32).sum(axis=0)


def joined_along(parts, dim):
    parts = jnp.moveaxis(parts, 0, dim)
    shape = parts.shape
    return parts.reshape(*shape[:dim], shape[dim] * shape[dim + 1], *shape[dim + 2 :])


def from_everyone(shard, axis):
    copies = jnp.broadcast_to(shard, (lax.axis_size(axis), *shard.shape))
    return lax.all_to_all(copies, axis, split_axis=0, concat_axis=0, tiled=True)


def gather_directly(shard, axis, dim):
    return joined_along(from_everyone(shard, axis), dim)


def per_device(hidden, down_weight, out_grad, pseudo_grad, momentum):
    token_rows = hidden[0]
    local_grads = out_grad[0]
    row_block = token_rows
    layer_out = sent_and_summed(
        jnp.dot(row_block, down_weight, preferred_element_type=jnp.float32).astype(jnp.bfloat16),
        "tp",
        0,
    ).astype(jnp.bfloat16)
    all_grads = gather_directly(local_grads, "tp", 0)
    row_block = all_grads
    hidden_grad = sent_and_summed(
        lax.dot_general(
            row_block, down_weight, (((1,), (1,)), ((), ())), preferred_element_type=jnp.float32
        ).astype(jnp.bfloat16),
        "dp",
        0,
    ).astype(jnp.bfloat16)
    replicas = lax.axis_size("rep")
    replica_terms = pseudo_grad[0].astype(jnp.float32)
    average = (
        lax.psum_scatter(
            replica_terms.astype(jnp.bfloat16), "rep", scatter_dimension=0, tiled=True
        ).astype(jnp.float32)
        / replicas
    )
    new_momentum = momentum_rate * momentum + average
    step_share = (outer_rate * (average + momentum_rate * new_momentum)).astype(jnp.bfloat16)
    outer_step = gather_directly(step_share, "rep", 0)
    return (layer_out[None], hidden_grad[None], new_momentum, outer_step)


def solution(mesh):
    return jax.shard_map(
        per_device,
        mesh=mesh,
        in_specs=(
            P("rep", None, "tp"),
            P("tp", "dp"),
            P("rep", "tp", "dp"),
            P("rep", "tp", "dp"),
            P(("tp", "rep"), "dp"),
        ),
        out_specs=(
            P("rep", "tp", "dp"),
            P("rep", "dp", "tp"),
            P(("tp", "rep"), "dp"),
            P("tp", "dp"),
        ),
        check_vma=False,
    )
```

profile of v0, /device:TPU:2, one launch (start us, length us, event | category | flops | bytes accessed | tf_op | source)
XLA Modules:
  0.0 180.9 jit_solution(13202091738954762791)
XLA Ops:
  7.2 0.0 copy-start
  7.2 1.8 broadcast_in_dim.13
  9.0 7.6 %all-to-all-start.1 = ((bf16[8,64,512]{2,1,0:T(8,128)(2,1)}), bf16[8,64,512]{2,1,0:T(8,128)(2,1)S(1)}, u32[]{:S(2)}, u32[]{:S(2)}) async-start(bf16[8,64,512]{2,1,0:T(8,128)(2,1)} %broadcast_in_dim.13), calls=%async_computation.1 | async-start | bytes 1048576 | tf_op jit(solution)/shard_map/all_to_all | solution.py:29
  16.5 0.0 copy-done
  16.6 3.4 %fusion.2 = bf16[512,512]{1,0:T(8,128)(2,1)} fusion(bf16[1792,512]{1,0:T(8,128)(2,1)S(1)} %copy-done, bf16[1,512,1792]{2,1,0:T(8,128)(2,1)} %param.5), kind=kOutput, calls=%fused_computation.3 | convolution fusion | flops 939786240 | bytes 4194304 | tf_op jit(solution)/shard_map/dot_general | solution.py:41
  20.0 14.1 %all-to-all-done.1 = bf16[8,64,512]{2,1,0:T(8,128)(2,1)S(1)} async-done(((bf16[8,64,512]{2,1,0:T(8,128)(2,1)}), bf16[8,64,512]{2,1,0:T(8,128)(2,1)S(1)}, u32[]{:S(2)}, u32[]{:S(2)}) %all-to-all-start.1) | async-done | bytes 524320 | tf_op jit(solution)/shard_map/all_to_all | solution.py:29
  34.0 3.5 %all-to-all-start = ((bf16[8,64,512]{2,1,0:T(8,128)(2,1)}), bf16[8,64,512]{2,1,0:T(8,128)(2,1)S(1)}, u32[]{:S(2)}, u32[]{:S(2)}) async-start(bf16[8,64,512]{2,1,0:T(8,128)(2,1)} %bitcast.1), calls=%async_computation | async-start | bytes 1048576 | tf_op jit(solution)/shard_map/all_to_all | solution.py:17
  37.5 0.0 reduce-scatter.2.cloned.1.call-start
  37.6 0.7 reduce-scatter.2.cloned.1.call-update
  38.3 2.4 %convolution_convert_fusion = bf16[512,1792]{1,0:T(8,128)(2,1)} fusion(bf16[512,512]{1,0:T(8,128)(2,1)S(1)} %bitcast.18, bf16[1792,512]{1,0:T(8,128)(2,1)S(1)} %copy-done), kind=kOutput, calls=%fused_computation | convolution fusion | flops 940441600 | bytes 4194304 | tf_op jit(solution)/shard_map/dot_general | solution.py:48
  40.7 14.7 %all-to-all-done = bf16[8,64,512]{2,1,0:T(8,128)(2,1)S(1)} async-done(((bf16[8,64,512]{2,1,0:T(8,128)(2,1)}), bf16[8,64,512]{2,1,0:T(8,128)(2,1)S(1)}, u32[]{:S(2)}, u32[]{:S(2)}) %all-to-all-start) | async-done | bytes 524320 | tf_op jit(solution)/shard_map/all_to_all | solution.py:17
  55.4 0.0 copy-start.1
  55.4 18.3 %all-to-all-start.2 = ((bf16[16,32,1792]{2,1,0:T(8,128)(2,1)}), bf16[16,32,1792]{2,1,0:T(8,128)(2,1)}, u32[]{:S(2)}, u32[]{:S(2)}) async-start(bf16[16,32,1792]{2,1,0:T(8,128)(2,1)} %bitcast.17), calls=%async_computation.2 | async-start | bytes 3670016 | tf_op jit(solution)/shard_map/all_to_all | solution.py:17
  73.7 34.5 %reduce-scatter.2.cloned.1.call-done = bf16[224,512]{1,0:T(8,128)(2,1)} async-done(((bf16[1792,512]{1,0:T(8,128)(2,1)}), bf16[224,512]{1,0:T(8,128)(2,1)}) %reduce-scatter.2.cloned.1.call-update) | async-done | bytes 229392 | tf_op jit(solution)/shard_map/reduce_scatter | solution.py:57
  108.2 0.0 copy-done.1
  108.2 1.8 %multiply_convert_fusion = (bf16[224,512]{1,0:T(8,128)(2,1)S(1)}, f32[224,512]{1,0:T(8,128)}) fusion(bf16[224,512]{1,0:T(8,128)(2,1)} %reduce-scatter.2.cloned.1.call-done, f32[224,512]{1,0:T(8,128)S(1)} %copy-done.1), kind=kLoop, calls=%fused_computation.4 | loop fusion | flops 917504 | bytes 1376256 | tf_op jit(solution)/shard_map/convert_element_type | solution.py:63
  110.0 8.2 %all-to-all-done.2 = bf16[16,32,1792]{2,1,0:T(8,128)(2,1)} async-done(((bf16[16,32,1792]{2,1,0:T(8,128)(2,1)}), bf16[16,32,1792]{2,1,0:T(8,128)(2,1)}, u32[]{:S(2)}, u32[]{:S(2)}) %all-to-all-start.2) | async-done | bytes 1835040 | tf_op jit(solution)/shard_map/all_to_all | solution.py:17
  118.2 1.4 broadcast_in_dim.15
  119.6 6.0 %all-to-all-start.3 = ((bf16[8,224,512]{2,1,0:T(8,128)(2,1)}), bf16[8,224,512]{2,1,0:T(8,128)(2,1)}, u32[]{:S(2)}, u32[]{:S(2)}) async-start(bf16[8,224,512]{2,1,0:T(8,128)(2,1)} %broadcast_in_dim.15), calls=%async_computation.4 | async-start | bytes 3670016 | tf_op jit(solution)/shard_map/all_to_all | solution.py:29
  125.6 0.7 reduce_sum.24
  126.3 2.4 %reduce_sum.25 = bf16[32,1792]{1,0:T(8,128)(2,1)} reduce(bf16[16,32,1792]{2,1,0:T(8,128)(2,1)} %all-to-all-done.2, bf16[]{:T(256)} %constant.3.clone.1), dimensions={0}, to_apply=%region_1.0 | reduce | flops 860160 | bytes 1949698 | tf_op jit(solution)/shard_map/reduce_sum | solution.py:18
  128.7 42.5 %all-to-all-done.3 = bf16[8,224,512]{2,1,0:T(8,128)(2,1)} async-done(((bf16[8,224,512]{2,1,0:T(8,128)(2,1)}), bf16[8,224,512]{2,1,0:T(8,128)(2,1)}, u32[]{:S(2)}, u32[]{:S(2)}) %all-to-all-start.3) | async-done | bytes 1835040 | tf_op jit(solution)/shard_map/all_to_all | solution.py:29
  171.2 2.8 %copy.10 = bf16[1792,512]{1,0:T(8,128)(2,1)} copy(bf16[1792,512]{1,0:T(8,128)(2,1)} %bitcast.8) | data formatting | bytes 3670016
Async XLA Ops:
  7.2 9.4 %copy-start = (bf16[1792,512]{1,0:T(8,128)(2,1)S(1)}, bf16[1792,512]{1,0:T(8,128)(2,1)}, u32[]{:S(2)}) copy-start(bf16[1792,512]{1,0:T(8,128)(2,1)} %param.6) | copy-start | bytes 5505028
  9.0 25.1 %all-to-all-start.1 = ((bf16[8,64,512]{2,1,0:T(8,128)(2,1)}), bf16[8,64,512]{2,1,0:T(8,128)(2,1)S(1)}, u32[]{:S(2)}, u32[]{:S(2)}) async-start(bf16[8,64,512]{2,1,0:T(8,128)(2,1)} %broadcast_in_dim.13), calls=%async_computation.1 | async-start | bytes 1048576 | tf_op jit(solution)/shard_map/all_to_all | solution.py:29
  34.0 21.4 %all-to-all-start = ((bf16[8,64,512]{2,1,0:T(8,128)(2,1)}), bf16[8,64,512]{2,1,0:T(8,128)(2,1)S(1)}, u32[]{:S(2)}, u32[]{:S(2)}) async-start(bf16[8,64,512]{2,1,0:T(8,128)(2,1)} %bitcast.1), calls=%async_computation | async-start | bytes 1048576 | tf_op jit(solution)/shard_map/all_to_all | solution.py:17
  37.5 70.6 %reduce-scatter.2.cloned.1.call-start = ((), (), s32[]{:S(2)}) async-start(), calls=%async_computation.5 | async-start | bytes 2064384 | tf_op jit(solution)/shard_map/reduce_scatter | solution.py:57
  55.4 52.8 %copy-start.1 = (f32[224,512]{1,0:T(8,128)S(1)}, f32[224,512]{1,0:T(8,128)}, u32[]{:S(2)}) copy-start(f32[224,512]{1,0:T(8,128)} %param.9) | copy-start | bytes 1376260
  55.4 62.8 %all-to-all-start.2 = ((bf16[16,32,1792]{2,1,0:T(8,128)(2,1)}), bf16[16,32,1792]{2,1,0:T(8,128)(2,1)}, u32[]{:S(2)}, u32[]{:S(2)}) async-start(bf16[16,32,1792]{2,1,0:T(8,128)(2,1)} %bitcast.17), calls=%async_computation.2 | async-start | bytes 3670016 | tf_op jit(solution)/shard_map/all_to_all | solution.py:17
  119.6 51.6 %all-to-all-start.3 = ((bf16[8,224,512]{2,1,0:T(8,128)(2,1)}), bf16[8,224,512]{2,1,0:T(8,128)(2,1)}, u32[]{:S(2)}, u32[]{:S(2)}) async-start(bf16[8,224,512]{2,1,0:T(8,128)(2,1)} %broadcast_in_dim.15), calls=%async_computation.4 | async-start | bytes 3670016 | tf_op jit(solution)/shard_map/all_to_all | solution.py:29
Sparse Core Ops, SparseCore 0:
  41.8 66.3 reduce-scatter.1
where the time goes:
time: 181 us
  waiting for transfers between devices  115 us (64%)
  starting transfers between devices  35.4 us (20%)
  between operations  14.1 us (8%)
  local copies, waits for them, and re-layouts  6.05 us (3%)
  matrix products  5.79 us (3%)
  other arithmetic  4.96 us (3%)
    all_to_all x2, waiting for transfers between devices, from_everyone(): return lax.all_to_all(copies, axis, split_axis=0, concat_axis=0, tiled=True)  56.6 us
    reduce_scatter x1, waiting for transfers between devices, per_device(): lax.psum_scatter(replica_terms.astype(jnp.bfloat16), 'rep', scatter_dimen...  34.5 us
    all_to_all x2, waiting for transfers between devices, sent_and_summed(): lax.all_to_all(parts, axis, split_axis=0, concat_axis=0, tiled=True)  22.9 us
    all_to_all x2, starting transfers between devices, sent_and_summed(): lax.all_to_all(parts, axis, split_axis=0, concat_axis=0, tiled=True)  21.8 us
    all_to_all x2, starting transfers between devices, from_everyone(): return lax.all_to_all(copies, axis, split_axis=0, concat_axis=0, tiled=True)  13.6 us
  transfers between devices with their start and end apart: 5, of which 5 were waited for; matrix products, arithmetic and copies ran while one was open for 6% of the time, Pallas kernels for 0%

commit v1 on v0

v1 whole, which is shorter than its diff:
```python
import functools

import jax
import jax.numpy as jnp
from jax import lax
from jax.experimental import pallas as pl
from jax.experimental.pallas import tpu as pltpu
from jax.sharding import PartitionSpec as P

outer_rate = 0.7
momentum_rate = 0.9
MESH = pl.DeviceIdType.MESH
F32, BF16 = jnp.float32, jnp.bfloat16
PIECES_X = 2
PIECES_Z = 2


def arm(n, sign, half):
    return n // 2 - (0 if (sign > 0) == (half == 0) else 1)


def ring_items(n, pieces):
    return [
        (s, h, d, c)
        for s in (1, -1)
        for h in (0, 1)
        for d in range(1, arm(n, s, h) + 1)
        for c in range(pieces)
    ]


def gather_plan(n):
    if n == 8:
        near = [(2, 0, 2), (-2, 0, 2), (1, 0, 2), (-1, 0, 2)]
        far = [(3, 2, 2), (-3, -2, 2), (4, 2, 0), (-4, -2, 1)]
        return near, far
    return [(o, 0, 2) for o in range(1, n)], []


def kernel(
    n_rep, n_dp, n_tp,
    hid, w, og, pg, mom,
    lay_o, hg_o, nm_o, out_o,
    hid_v, w_v, og_v, pgo, pgm, mom_v, dd, xr, outv, nm_v,
    po, lrecv, lay_v, part, brecv, fin, xs, xrv, hg_v,
    load_sem, dd_sem, rs_sem, ag_sem, pass_sem, put_sem, g_sem, l_sem, b_sem, e_sem, o_sem,
):
    n_x, n_z, n_y = n_rep // 2, n_dp // 2, n_tp
    rep, dp, y = lax.axis_index("rep"), lax.axis_index("dp"), lax.axis_index("tp")
    x, core = rep // 2, rep % 2
    z, low = dp // 2, dp % 2
    width = w.shape[1]
    units = w.shape[0]
    shift = n_z // 2 - 1

    def at_x(k):
        return lax.rem(x + k % n_x, n_x)

    def to_x(s):
        return {"rep": 2 * at_x(s) + core}

    def to_z(s):
        return {"dp": 2 * lax.rem(z + s % n_z, n_z) + low}

    def to_y(o):
        return {"tp": lax.rem(y + o % n_y, n_y)}

    partner = {"rep": 2 * x + 1 - core}
    pair = {"dp": 2 * z + 1 - low}

    def remote(src, dst, sems, i, where):
        return pltpu.make_async_remote_copy(
            src_ref=src, dst_ref=dst, send_sem=sems.at[0, i], recv_sem=sems.at[1, i],
            device_id=where, device_id_type=MESH,
        )

    def span(total, pieces, c):
        return pl.ds(c * (total // pieces), total // pieces)

    sent = []

    def go(copy):
        copy.start()
        sent.append(copy)
        return copy

    order_x = sorted(range(n_x), key=lambda k: -min(k, n_x - k))
    slot_me = lax.rem(y + (-shift) % n_z + n_z - z, n_z)
    loads = {}

    def load(name, src, dst):
        loads[name] = pltpu.make_async_copy(src, dst, load_sem.at[len(loads)])
        loads[name].start()

    load("og", og, og_v.at[slot_me])
    for k in order_x:
        load(("o", k), pg.at[2 * at_x(k) + 1 - core], pgo.at[k])
    for k in order_x:
        load(("m", k), pg.at[2 * at_x(k) + core], pgm.at[k])
    load("w", w, w_v)
    load("hid", hid, hid_v)
    load("mom", mom, mom_v)

    peers = [partner, pair]
    peers += [to_x(s) for s in sorted({1 % n_x, -1 % n_x} - {0})]
    peers += [to_z(s) for s in sorted({1 % n_z, -1 % n_z} - {0})]
    peers += [to_y(o) for o in range(1, n_y)]
    barrier = pltpu.get_barrier_semaphore()
    for where in peers:
        pl.semaphore_signal(barrier, inc=1, device_id=where, device_id_type=MESH)
    pl.semaphore_wait(barrier, len(peers))

    near, far = gather_plan(n_y)
    g_index = {o: i for i, (o, _, _) in enumerate(near + far)}
    gathers = {}
    half_rows = og.shape[0] // 2

    def gather(o, relay, rows):
        slot = lax.rem(slot_me + (-relay) % n_z, n_z)
        ref = og_v.at[slot]
        if rows < 2:
            ref = ref.at[pl.ds(rows * half_rows, half_rows)]
        gathers[o] = go(remote(ref, ref, g_sem, g_index[o], to_y(o - relay)))

    loads["og"].wait()
    for o, relay, rows in near:
        gather(o, relay, rows)
    swaps = {}
    for k in order_x:
        loads["o", k].wait()
        swaps[k] = go(remote(pgo.at[k], dd.at[k], dd_sem, k, partner))

    ready = set()

    def have(k):
        if k not in ready:
            ready.add(k)
            swaps[k].wait_recv()
            loads["m", k].wait()

    x_items = ring_items(n_x, PIECES_X)
    x_index = {key: i for i, key in enumerate(x_items)}
    rs = {}

    def sign_at(s):
        return 0 if s > 0 else 1

    def rs_send(s, h, d, c):
        k = (s * d) % n_x
        cols = span(width, PIECES_X, c)
        total = pgm[k, h, :, cols].astype(F32) + dd[k, h, :, cols].astype(F32)
        if d < arm(n_x, s, h):
            rs[s, h, d + 1, c].wait_recv()
            total = total + xr[sign_at(s), h, d, :, cols].astype(F32)
        dd[k, h, :, cols] = total.astype(BF16)
        rs[s, h, d, c] = go(
            remote(dd.at[k, h, :, cols], xr.at[sign_at(s), h, d - 1, :, cols], rs_sem, x_index[s, h, d, c], to_x(s))
        )

    ag = {}

    def ag_send(s, h, d, c):
        cols = span(width, PIECES_X, c)
        ag[s, h, d, c] = go(
            remote(
                outv.at[(-s * (d - 1)) % n_x, h, :, cols], outv.at[(-s * d) % n_x, h, :, cols],
                ag_sem, x_index[s, h, d, c], to_x(s),
            )
        )

    passed, puts = [], []

    def hand_out(k, h, c):
        cols = span(width, PIECES_X, c)
        i = (k * 2 + h) * PIECES_X + c
        home = out_o.at[2 * at_x(k) + core, h, :, cols]
        passed.append(go(remote(outv.at[k, h, :, cols], home, pass_sem, i, partner)))
        put = pltpu.make_async_copy(outv.at[k, h, :, cols], home, put_sem.at[i])
        put.start()
        puts.append(put)

    def rs_end(c):
        have(0)
        cols = span(width, PIECES_X, c)
        for h in (0, 1):
            total = pgm[0, h, :, cols].astype(F32) + dd[0, h, :, cols].astype(F32)
            for s in (1, -1):
                if arm(n_x, s, h) >= 1:
                    rs[s, h, 1, c].wait_recv()
                    total = total + xr[sign_at(s), h, 0, :, cols].astype(F32)
            average = total * (1.0 / n_rep)
            new = momentum_rate * mom_v[h, :, cols] + average
            nm_v[h, :, cols] = new
            outv[0, h, :, cols] = (outer_rate * (average + momentum_rate * new)).astype(BF16)
        for far_first in (True, False):
            for s in (1, -1):
                for h in (0, 1):
                    if arm(n_x, s, h) >= 1 and ((s > 0) == (h == 0)) == far_first:
                        ag_send(s, h, 1, c)
        for h in (0, 1):
            hand_out(0, h, c)

    def ag_take(s, h, d, c):
        ag[s, h, d, c].wait_recv()
        if d < arm(n_x, s, h):
            ag_send(s, h, d + 1, c)
        hand_out((-s * d) % n_x, h, c)

    starts = []
    for c in range(PIECES_X):
        for s in (1, -1):
            for h in (0, 1):
                d = arm(n_x, s, h)
                if d >= 1:
                    starts.append((c, -d, s, h, d))
    for c, _, s, h, d in sorted(starts):
        have((s * d) % n_x)
        rs_send(s, h, d, c)

    loads["w"].wait()
    loads["hid"].wait()
    tile = min(256, width)

    @pl.loop(0, width // tile)
    def _(j):
        cols = pl.ds(pl.multiple_of(j * tile, tile), tile)
        block = jnp.dot(hid_v[...], w_v[:, cols], preferred_element_type=F32)
        po[:, :, cols] = block.astype(BF16).reshape(n_y, -1, tile)

    relayed = set()
    for o, relay, rows in far:
        if relay not in relayed:
            relayed.add(relay)
            gathers[relay].wait_recv()
        gather(o, relay, rows)

    def rs_rest(c):
        for d in range(n_x // 2 - 1, 0, -1):
            for s in (1, -1):
                for h in (0, 1):
                    if d < arm(n_x, s, h):
                        rs_send(s, h, d, c)

    for c in range(PIECES_X):
        rs_rest(c)

    for o in gathers:
        if o not in relayed:
            gathers[o].wait_recv()

    outs = []
    exchange = {}
    for o in range(1, n_y):
        exchange[o] = go(remote(po.at[lax.rem(y + o, n_y)], lrecv.at[o - 1], l_sem, o - 1, to_y(o)))

    f_tile = min(256, units)

    def back(a, b):
        @pl.loop(0, units // f_tile)
        def _(j):
            cols = pl.ds(pl.multiple_of(j * f_tile, f_tile), f_tile)
            rows = og_v[pl.ds(a, b - a)].reshape(-1, width)
            block = lax.dot_general(rows, w_v[cols, :], (((1,), (1,)), ((), ())), preferred_element_type=F32)
            part[pl.ds(a, b - a), :, :, cols] = block.astype(BF16).reshape(b - a, 2, -1, f_tile)

    z_items = ring_items(n_z, PIECES_Z)
    z_index = {key: i for i, key in enumerate(z_items)}
    zs = {}

    def z_slot(k):
        return (k - shift) % n_z

    def z_send(s, h, d, c):
        k = z_slot(s * d)
        cols = span(units, PIECES_Z, c)
        if d < arm(n_z, s, h):
            zs[s, h, d + 1, c].wait_recv()
            total = part[k, h, :, cols].astype(F32) + brecv[sign_at(s), h, d, :, cols].astype(F32)
            part[k, h, :, cols] = total.astype(BF16)
        zs[s, h, d, c] = go(
            remote(part.at[k, h, :, cols], brecv.at[sign_at(s), h, d - 1, :, cols], b_sem, z_index[s, h, d, c], to_z(s))
        )

    def z_wave(step, long_arm):
        for c in range(PIECES_Z):
            for s in (1, -1):
                h = 0 if (s > 0) == long_arm else 1
                d = arm(n_z, s, h) - step
                if d >= 1:
                    z_send(s, h, d, c)

    cut = min(3, n_z)
    back(0, cut)
    z_wave(0, True)
    z_wave(0, False)
    if cut < n_z:
        back(cut, n_z)

    ends = {}

    def z_end(c):
        cols = span(units, PIECES_Z, c)
        for h in (0, 1):
            total = part[z_slot(0), h, :, cols].astype(F32)
            for s in (1, -1):
                if arm(n_z, s, h) >= 1:
                    zs[s, h, 1, c].wait_recv()
                    total = total + brecv[sign_at(s), h, 0, :, cols].astype(F32)
            fin[h, :, cols] = total
        xs[:, cols] = fin[1 - low, :, cols].astype(BF16)
        ends[c] = go(remote(xs.at[:, cols], xrv.at[:, cols], e_sem, c, pair))

    def grad_out(c):
        cols = span(units, PIECES_Z, c)
        ends[c].wait_recv()
        hg_v[:, cols] = (fin[low, :, cols] + xrv[:, cols].astype(F32)).astype(BF16)
        put(hg_v.at[:, cols], hg_o.at[:, cols])

    def put(src, dst):
        copy = pltpu.make_async_copy(src, dst, o_sem.at[len(outs)])
        copy.start()
        outs.append(copy)

    def layer_out():
        total = po[y].astype(F32)
        for o in range(1, n_y):
            exchange[o].wait_recv()
            total = total + lrecv[o - 1].astype(F32)
        lay_v[...] = total.astype(BF16)
        put(lay_v, lay_o)

    def takes(d, c):
        for s in (1, -1):
            for h in (0, 1):
                if d <= arm(n_x, s, h):
                    ag_take(s, h, d, c)

    loads["mom"].wait()
    rs_end(0)
    z_wave(1, True)
    for c in range(1, PIECES_X):
        rs_end(c)
    put(nm_v, nm_o)
    z_wave(1, False)
    for c in range(PIECES_X):
        takes(1, c)
        z_wave(2, c == 0)
    for step in range(3, n_z // 2):
        z_wave(step, True)
        z_wave(step, False)
    layer_out()
    for c in range(PIECES_Z):
        z_end(c)
    for d in range(2, n_x // 2 + 1):
        for c in range(PIECES_X):
            takes(d, c)
    for c in range(PIECES_Z):
        grad_out(c)
    for copy in passed:
        copy.wait_recv()
    for copy in sent:
        copy.wait_send()
    for copy in puts + outs:
        copy.wait()


def per_device(sizes, hidden, down_weight, out_grad, pseudo_grad, momentum):
    n_rep, n_dp, n_tp = sizes
    n_x, n_z = n_rep // 2, n_dp // 2
    tokens, units = hidden.shape[1:]
    width = down_weight.shape[1]
    rows = out_grad.shape[1]
    share = momentum.shape[0] // 2
    owned = tokens // n_dp
    far_x, far_z = max(n_x // 2, 1), max(n_z // 2, 1)
    x_copies = max(len(ring_items(n_x, PIECES_X)), 1)
    z_copies = max(len(ring_items(n_z, PIECES_Z)), 1)
    near, far = gather_plan(n_tp)
    any_ref = pl.BlockSpec(memory_space=pl.ANY)
    sem = pltpu.SemaphoreType.DMA
    lay, hg, nm, out = pl.pallas_call(
        functools.partial(kernel, n_rep, n_dp, n_tp),
        out_shape=(
            jax.ShapeDtypeStruct((rows, width), BF16),
            jax.ShapeDtypeStruct((owned, units), BF16),
            jax.ShapeDtypeStruct((2, share, width), F32),
            jax.ShapeDtypeStruct((n_rep, 2, share, width), BF16),
        ),
        in_specs=[any_ref] * 5,
        out_specs=(any_ref,) * 4,
        scratch_shapes=[
            pltpu.VMEM((tokens, units), BF16),
            pltpu.VMEM((units, width), BF16),
            pltpu.VMEM((n_tp, rows, width), BF16),
            pltpu.VMEM((n_x, 2, share, width), BF16),
            pltpu.VMEM((n_x, 2, share, width), BF16),
            pltpu.VMEM((2, share, width), F32),
            pltpu.VMEM((n_x, 2, share, width), BF16),
            pltpu.VMEM((2, 2, far_x, share, width), BF16),
            pltpu.VMEM((n_x, 2, share, width), BF16),
            pltpu.VMEM((2, share, width), F32),
            pltpu.VMEM((n_tp, rows, width), BF16),
            pltpu.VMEM((max(n_tp - 1, 1), rows, width), BF16),
            pltpu.VMEM((rows, width), BF16),
            pltpu.VMEM((n_z, 2, owned, units), BF16),
            pltpu.VMEM((2, 2, far_z, owned, units), BF16),
            pltpu.VMEM((2, owned, units), F32),
            pltpu.VMEM((owned, units), BF16),
            pltpu.VMEM((owned, units), BF16),
            pltpu.VMEM((owned, units), BF16),
            sem((4 + 2 * n_x,)),
            sem((2, n_x)),
            sem((2, x_copies)),
            sem((2, x_copies)),
            sem((2, 2 * n_x * PIECES_X)),
            sem((2 * n_x * PIECES_X,)),
            sem((2, max(len(near + far), 1))),
            sem((2, max(n_tp - 1, 1))),
            sem((2, z_copies)),
            sem((2, PIECES_Z)),
            sem((2 + PIECES_Z,)),
        ],
        compiler_params=pltpu.CompilerParams(collective_id=0, has_side_effects=True),
        name="step",
    )(
        hidden[0],
        down_weight,
        out_grad[0],
        pseudo_grad.reshape(n_rep, 2, share, width),
        momentum.reshape(2, share, width),
    )
    return lay[None], hg[None], nm.reshape(momentum.shape), out.reshape(down_weight.shape)


def solution(mesh):
    sizes = tuple(mesh.shape[axis] for axis in ("rep", "dp", "tp"))
    return jax.shard_map(
        functools.partial(per_device, sizes),
        mesh=mesh,
        in_specs=(
            P("rep", None, "tp"),
            P("tp", "dp"),
            P("rep", "tp", "dp"),
            P("rep", "tp", "dp"),
            P(("tp", "rep"), "dp"),
        ),
        out_specs=(
            P("rep", "tp", "dp"),
            P("rep", "dp", "tp"),
            P(("tp", "rep"), "dp"),
            P("tp", "dp"),
        ),
        check_vma=False,
    )
```

time: 181 us -> 77.1 us (0.43)
  the two profiles are of different devices: /device:TPU:2 before, /device:TPU:1 now
where the time goes in v1:
time: 77.1 us; the launch traced here: 76.8 us
  Pallas kernels  68.5 us (89%)
  local copies, waits for them, and re-layouts  7.68 us (10%)
    pallas_call x1, Pallas kernels, per_device(): pl.pallas_call(functools.partial(kernel, n_rep, n_dp, n_tp), out_shape=(j...  68.5 us
    unnamed x4, local copies, waits for them, and re-layouts  7.68 us

profile of v1, /device:TPU:1, one launch (start us, length us, event | category | flops | bytes accessed | tf_op | source)
XLA Modules:
  0.0 76.8 jit_solution(248322601452694205)
XLA Ops:
  0.6 68.5 %step.1 = (bf16[64,512]{1,0:T(8,128)(2,1)}, bf16[32,1792]{1,0:T(8,128)(2,1)}, f32[2,112,512]{2,1,0:T(8,128)}, bf16[8,2,112,512]{3,2,1,0:T(8,128)(2,1)}) custom-call(bf16[512,1792]{1,0:T(8,128)(2,1)} %bitcast.9, bf16[1792,512]{1,0:T(8,128)(2,1)} %w.1, bf16[64,512]{1,0:T(8,128)(2,1)} %bitcast.14, bf16[8,2,112,512]{3,2,1,0:T(8,128)(2,1)} %bitcast.10, ...), custom_call_target="tpu_custom_call" | custom-call | tf_op jit(solution)/shard_map/step/pallas_call | solution.py:381
  69.1 1.5 %copy.13 = bf16[1,64,512]{2,1,0:T(8,128)(2,1)} copy(bf16[1,64,512]{2,1,0:T(8,128)(2,1)} %bitcast.15) | data formatting | bytes 131072
  70.6 1.6 %copy.14 = bf16[1,32,1792]{2,1,0:T(8,128)(2,1)} copy(bf16[1,32,1792]{2,1,0:T(8,128)(2,1)} %bitcast.13) | data formatting | bytes 229376
  72.1 1.8 %copy.15 = f32[224,512]{1,0:T(8,128)} copy(f32[224,512]{1,0:T(8,128)} %bitcast.12) | data formatting | bytes 917504
  73.9 2.8 %copy.16 = bf16[1792,512]{1,0:T(8,128)(2,1)} copy(bf16[1792,512]{1,0:T(8,128)(2,1)} %bitcast.8) | data formatting | bytes 3670016

commit v2 on v0

v2 whole, which is shorter than its diff:
```python
import functools

import jax
import jax.numpy as jnp
from jax import lax
from jax.experimental import pallas as pl
from jax.experimental.pallas import tpu as pltpu
from jax.sharding import PartitionSpec as P

outer_rate = 0.7
momentum_rate = 0.9
MESH = pl.DeviceIdType.MESH
F32, BF16 = jnp.float32, jnp.bfloat16
PIECES_X = 2
PIECES_Z = 2


def arm(n, sign, half):
    return n // 2 - (0 if (sign > 0) == (half == 0) else 1)


def ring_items(n, pieces):
    return [
        (s, h, d, c)
        for s in (1, -1)
        for h in (0, 1)
        for d in range(1, arm(n, s, h) + 1)
        for c in range(pieces)
    ]


def gather_plan(n):
    if n == 8:
        near = [(2, 0, 2), (-2, 0, 2), (1, 0, 2), (-1, 0, 2)]
        far = [(4, 2, 0), (-4, -2, 1), (3, 2, 2), (-3, -2, 2)]
        return near, far
    return [(o, 0, 2) for o in range(1, n)], []


def kernel(
    n_rep, n_dp, n_tp,
    hid, w, og, pg, mom,
    lay_o, hg_o, nm_o, out_o,
    pgm, dd, xr, mom_v, nm_v,
    hid_v, w_v, wt_v, og_v, po, lrecv, lay_v, part, brecv, fin, xs, xrv, hg_v,
    load_sem, give_sem, rs_sem, ag_sem, pass_sem, g_sem, l_sem, b_sem, e_sem, h_sem, z_sem,
):
    n_x, n_z, n_y = n_rep // 2, n_dp // 2, n_tp
    rep, dp, y = lax.axis_index("rep"), lax.axis_index("dp"), lax.axis_index("tp")
    x, core = rep // 2, rep % 2
    z, low = dp // 2, dp % 2
    units, width = w.shape
    shift = n_z // 2 - 1
    slot_me = lax.rem(y + (-shift) % n_z + n_z - z, n_z)
    partner = {"rep": 2 * x + 1 - core}
    pair = {"dp": 2 * z + 1 - low}
    order_x = sorted(range(n_x), key=lambda k: -min(k, n_x - k))
    barrier = pltpu.get_barrier_semaphore()

    def at_x(k):
        return lax.rem(x + k % n_x, n_x)

    def to_x(s):
        return {"rep": 2 * at_x(s) + core}

    def to_z(s):
        return {"dp": 2 * lax.rem(z + s % n_z, n_z) + low}

    def to_y(o):
        return {"tp": lax.rem(y + o % n_y, n_y)}

    def remote(src, dst, sems, i, where):
        return pltpu.make_async_remote_copy(
            src_ref=src, dst_ref=dst, send_sem=sems.at[0, i], recv_sem=sems.at[1, i],
            device_id=where, device_id_type=MESH,
        )

    def arrived(ref, sems, i):
        remote(ref, ref, sems, i, partner).wait_recv()

    def span(total, pieces, c):
        return pl.ds(c * (total // pieces), total // pieces)

    def sign_at(s):
        return 0 if s > 0 else 1

    def greet(peers):
        for where in peers:
            pl.semaphore_signal(barrier, inc=1, device_id=where, device_id_type=MESH)

    MOM, OG, HID, NM, LAY = range(n_x, n_x + 5)

    def x_program():
        sent, loads = [], {}

        def go(copy):
            copy.start()
            sent.append(copy)
            return copy

        def load(name, src, dst):
            loads[name] = pltpu.make_async_copy(src, dst, load_sem.at[len(loads)])
            loads[name].start()

        for k in order_x:
            load(k, pg.at[at_x(k)], pgm.at[k])
        load("mom", mom, mom_v.at[0])
        peers = [partner] + [to_x(s) for s in sorted({1 % n_x, -1 % n_x} - {0})]
        greet(peers)
        pl.semaphore_wait(barrier, len(peers))
        go(remote(og, og_v.at[0, slot_me], give_sem, OG, partner))
        go(remote(hid, hid_v.at[0], give_sem, HID, partner))

        index = {key: i for i, key in enumerate(ring_items(n_x, PIECES_X))}
        rs, ag, ready = {}, {}, set()

        def have(k):
            if k not in ready:
                ready.add(k)
                arrived(dd.at[k], give_sem, k)
                loads[k].wait()

        def rs_send(s, h, d, c):
            k = (s * d) % n_x
            cols = span(width, PIECES_X, c)
            total = pgm[k, h, :, cols].astype(F32) + dd[k, h, :, cols].astype(F32)
            if d < arm(n_x, s, h):
                rs[s, h, d + 1, c].wait_recv()
                total = total + xr[sign_at(s), h, d, :, cols].astype(F32)
            dd[k, h, :, cols] = total.astype(BF16)
            target = xr.at[sign_at(s), h, d - 1, :, cols]
            rs[s, h, d, c] = go(remote(dd.at[k, h, :, cols], target, rs_sem, index[s, h, d, c], to_x(s)))

        def hand_out(k, h, c):
            piece = out_o.at[at_x(k), h, :, span(width, PIECES_X, c)]
            go(remote(piece, piece, pass_sem, (k * 2 + h) * PIECES_X + c, partner))

        def ag_send(s, h, d, c):
            piece = out_o.at[at_x(-s * (d - 1)), h, :, span(width, PIECES_X, c)]
            ag[s, h, d, c] = go(remote(piece, piece, ag_sem, index[s, h, d, c], to_x(s)))

        def ag_take(s, h, d, c):
            ag[s, h, d, c].wait_recv()
            if d < arm(n_x, s, h):
                ag_send(s, h, d + 1, c)
            hand_out((-s * d) % n_x, h, c)

        def rs_end(c):
            have(0)
            cols = span(width, PIECES_X, c)
            for h in (0, 1):
                total = pgm[0, h, :, cols].astype(F32) + dd[0, h, :, cols].astype(F32)
                for s in (1, -1):
                    if arm(n_x, s, h) >= 1:
                        rs[s, h, 1, c].wait_recv()
                        total = total + xr[sign_at(s), h, 0, :, cols].astype(F32)
                average = total * (1.0 / n_rep)
                new = momentum_rate * mom_v[h, :, cols] + average
                if h == 0:
                    nm_o[:, cols] = new
                else:
                    nm_v[:, cols] = new
                out_o[x, h, :, cols] = (outer_rate * (average + momentum_rate * new)).astype(BF16)
            for far_first in (True, False):
                for s in (1, -1):
                    for h in (0, 1):
                        if arm(n_x, s, h) >= 1 and ((s > 0) == (h == 0)) == far_first:
                            ag_send(s, h, 1, c)
            for h in (0, 1):
                hand_out(0, h, c)

        starts = sorted(
            (c, -arm(n_x, s, h), s, h)
            for c in range(PIECES_X)
            for s in (1, -1)
            for h in (0, 1)
            if arm(n_x, s, h) >= 1
        )
        for c, d, s, h in starts:
            have((s * -d) % n_x)
            rs_send(s, h, -d, c)
        for c in range(PIECES_X):
            for d in range(n_x // 2 - 1, 0, -1):
                for s in (1, -1):
                    for h in (0, 1):
                        if d < arm(n_x, s, h):
                            rs_send(s, h, d, c)
        loads["mom"].wait()
        arrived(mom_v.at[1], give_sem, MOM)
        for c in range(PIECES_X):
            rs_end(c)
        go(remote(nm_v, nm_o, give_sem, NM, partner))
        for d in range(1, n_x // 2 + 1):
            for c in range(PIECES_X):
                for s in (1, -1):
                    for h in (0, 1):
                        if d <= arm(n_x, s, h):
                            ag_take(s, h, d, c)
        arrived(lay_o, give_sem, LAY)
        for c in range(PIECES_Z):
            arrived(hg_o.at[:, span(units, PIECES_Z, c)], h_sem, c)
        for copy in sent:
            copy.wait_send()

    def z_program():
        sent, loads = [], {}

        def go(copy):
            copy.start()
            sent.append(copy)
            return copy

        def load(name, src, dst):
            loads[name] = pltpu.make_async_copy(src, dst, load_sem.at[len(loads)])
            loads[name].start()

        load("og", og, og_v.at[1, slot_me])
        load("w", w, w_v)
        load("hid", hid, hid_v.at[1])

        peers = [partner, pair] + [to_y(o) for o in range(1, n_y)]
        greet(peers)
        lower_than = {1: z < n_z - 1, -1: z == 0}
        higher_than = {1: z == n_z - 1, -1: z > 0}
        if n_z > 1:
            for s in (1, -1):

                @pl.when(lower_than[s])
                def _():
                    greet([to_z(s)])

            pl.semaphore_wait(barrier, len(peers) + (z + n_z - 1) // n_z + (z + 1) // n_z)
            for s in (1, -1):

                @pl.when(higher_than[s])
                def _():
                    pl.semaphore_signal(z_sem.at[sign_at(-s)], inc=1, device_id=to_z(s), device_id_type=MESH)

        else:
            pl.semaphore_wait(barrier, len(peers))

        near, far = gather_plan(n_y)
        g_index = {(o, r): 2 * i + r for i, (o, _, _) in enumerate(near + far) for r in (0, 1)}
        gathers, relayed = {}, set()
        half_rows = og.shape[0] // 2

        def gather(o, relay, rows, r):
            if relay and (relay, r) not in relayed:
                relayed.add((relay, r))
                gathers[relay, r].wait_recv()
            ref = og_v.at[r, lax.rem(slot_me + (-relay) % n_z, n_z)]
            if rows < 2:
                ref = ref.at[pl.ds(rows * half_rows, half_rows)]
            gathers[o, r] = go(remote(ref, ref, g_sem, g_index[o, r], to_y(o - relay)))

        loads["og"].wait()
        for item in near:
            gather(*item, 1)
        for k in order_x:
            go(remote(pg.at[at_x(k)], dd.at[k], give_sem, k, partner))
        go(remote(mom, mom_v.at[1], give_sem, MOM, partner))
        arrived(og_v.at[0, slot_me], give_sem, OG)
        for item in near:
            gather(*item, 0)

        loads["w"].wait()
        f_tile = min(256, units)

        @pl.loop(0, units // f_tile)
        def _(j):
            cols = pl.ds(pl.multiple_of(j * f_tile, f_tile), f_tile)
            wt_v[:, cols] = w_v[cols, :].T

        for r in (1, 0):
            for item in far:
                gather(*item, r)

        loads["hid"].wait()
        arrived(hid_v.at[0], give_sem, HID)
        tile = min(256, width)

        @pl.loop(0, width // tile)
        def _(j):
            cols = pl.ds(pl.multiple_of(j * tile, tile), tile)
            for r in (0, 1):
                block = jnp.dot(hid_v[r], w_v[:, cols], preferred_element_type=F32)
                po[:, r, :, cols] = block.astype(BF16).reshape(n_y, -1, tile)

        for key in gathers:
            if key not in relayed:
                gathers[key].wait_recv()

        exchange = {}
        for o in range(1, n_y):
            exchange[o] = go(remote(po.at[lax.rem(y + o, n_y)], lrecv.at[o - 1], l_sem, o - 1, to_y(o)))

        def back(a, b):
            @pl.loop(0, units // f_tile)
            def _(j):
                cols = pl.ds(pl.multiple_of(j * f_tile, f_tile), f_tile)
                rows = og_v[:, pl.ds(a, b - a)].reshape(-1, width)
                block = jnp.dot(rows, wt_v[:, cols], preferred_element_type=F32).astype(BF16)
                block = block.reshape(2, b - a, 2, -1, f_tile)
                for r in (0, 1):
                    part[pl.ds(a, b - a), :, r, :, cols] = block[r]

        z_index = {key: i for i, key in enumerate(ring_items(n_z, PIECES_Z))}
        zs = {}

        def z_slot(k):
            return (k - shift) % n_z

        def z_send(s, h, d, c):
            k = z_slot(s * d)
            cols = span(units, PIECES_Z, c)
            if d < arm(n_z, s, h):
                zs[s, h, d + 1, c].wait_recv()
                total = part[k, h, :, :, cols].astype(F32) + brecv[sign_at(s), h, d, :, :, cols].astype(F32)
                part[k, h, :, :, cols] = total.astype(BF16)
            target = brecv.at[sign_at(s), h, d - 1, :, :, cols]
            zs[s, h, d, c] = go(remote(part.at[k, h, :, :, cols], target, b_sem, z_index[s, h, d, c], to_z(s)))

        def z_wave(step, long_arm):
            for c in range(PIECES_Z):
                for s in (1, -1):
                    h = 0 if (s > 0) == long_arm else 1
                    d = arm(n_z, s, h) - step
                    if d >= 1:
                        z_send(s, h, d, c)

        cut = min(3, n_z)
        back(0, cut)
        if n_z > 1:
            for s in (1, -1):

                @pl.when(lower_than[s])
                def _():
                    pl.semaphore_wait(z_sem.at[sign_at(s)], 1)

        z_wave(0, True)
        z_wave(0, False)
        if cut < n_z:
            back(cut, n_z)
        for step in range(1, n_z // 2):
            z_wave(step, True)
            z_wave(step, False)

        ends = {}
        for c in range(PIECES_Z):
            cols = span(units, PIECES_Z, c)
            for h in (0, 1):
                total = part[z_slot(0), h, :, :, cols].astype(F32)
                for s in (1, -1):
                    if arm(n_z, s, h) >= 1:
                        zs[s, h, 1, c].wait_recv()
                        total = total + brecv[sign_at(s), h, 0, :, :, cols].astype(F32)
                fin[h, :, :, cols] = total
            xs[:, :, cols] = fin[1 - low, :, :, cols].astype(BF16)
            ends[c] = go(remote(xs.at[:, :, cols], xrv.at[:, :, cols], e_sem, c, pair))

        total = po[y].astype(F32)
        for o in range(1, n_y):
            exchange[o].wait_recv()
            total = total + lrecv[o - 1].astype(F32)
        lay_v[...] = total[0].astype(BF16)
        lay_o[...] = total[1].astype(BF16)
        go(remote(lay_v, lay_o, give_sem, LAY, partner))

        for c in range(PIECES_Z):
            cols = span(units, PIECES_Z, c)
            ends[c].wait_recv()
            total = fin[low, :, :, cols] + xrv[:, :, cols].astype(F32)
            hg_v[:, cols] = total[0].astype(BF16)
            hg_o[:, cols] = total[1].astype(BF16)
            go(remote(hg_v.at[:, cols], hg_o.at[:, cols], h_sem, c, partner))

        for k in range(n_x):
            for h in (0, 1):
                for c in range(PIECES_X):
                    piece = out_o.at[at_x(k), h, :, span(width, PIECES_X, c)]
                    arrived(piece, pass_sem, (k * 2 + h) * PIECES_X + c)
        arrived(nm_o, give_sem, NM)
        for copy in sent:
            copy.wait_send()

    pl.when(core == 0)(x_program)
    pl.when(core == 1)(z_program)


def store(*refs):
    copies = [pltpu.make_async_copy(refs[i], refs[4 + i], refs[8].at[i]) for i in range(4)]
    for copy in copies:
        copy.start()
    for copy in copies:
        copy.wait()


def per_device(sizes, hidden, down_weight, out_grad, pseudo_grad, momentum):
    n_rep, n_dp, n_tp = sizes
    n_x, n_z = n_rep // 2, n_dp // 2
    tokens, units = hidden.shape[1:]
    width = down_weight.shape[1]
    rows = out_grad.shape[1]
    share = momentum.shape[0]
    owned = tokens // n_dp
    far_x, far_z = max(n_x // 2, 1), max(n_z // 2, 1)
    x_copies = max(len(ring_items(n_x, PIECES_X)), 1)
    z_copies = max(len(ring_items(n_z, PIECES_Z)), 1)
    near, far = gather_plan(n_tp)
    any_ref = pl.BlockSpec(memory_space=pl.ANY)
    vmem = pl.BlockSpec(memory_space=pltpu.VMEM)
    sem = pltpu.SemaphoreType.DMA
    results = pl.pallas_call(
        functools.partial(kernel, n_rep, n_dp, n_tp),
        out_shape=(
            pltpu.VMEM((rows, width), BF16),
            pltpu.VMEM((owned, units), BF16),
            pltpu.VMEM((share, width), F32),
            pltpu.VMEM((n_x, 2, share, width), BF16),
        ),
        in_specs=[any_ref] * 5,
        out_specs=(vmem,) * 4,
        scratch_shapes=[
            pltpu.VMEM((n_x, 2, share, width), BF16),
            pltpu.VMEM((n_x, 2, share, width), BF16),
            pltpu.VMEM((2, 2, far_x, share, width), BF16),
            pltpu.VMEM((2, share, width), F32),
            pltpu.VMEM((share, width), F32),
            pltpu.VMEM((2, tokens, units), BF16),
            pltpu.VMEM((units, width), BF16),
            pltpu.VMEM((width, units), BF16),
            pltpu.VMEM((2, n_tp, rows, width), BF16),
            pltpu.VMEM((n_tp, 2, rows, width), BF16),
            pltpu.VMEM((max(n_tp - 1, 1), 2, rows, width), BF16),
            pltpu.VMEM((rows, width), BF16),
            pltpu.VMEM((n_z, 2, 2, owned, units), BF16),
            pltpu.VMEM((2, 2, far_z, 2, owned, units), BF16),
            pltpu.VMEM((2, 2, owned, units), F32),
            pltpu.VMEM((2, owned, units), BF16),
            pltpu.VMEM((2, owned, units), BF16),
            pltpu.VMEM((owned, units), BF16),
            sem((max(n_x + 1, 3),)),
            sem((2, n_x + 5)),
            sem((2, x_copies)),
            sem((2, x_copies)),
            sem((2, 2 * n_x * PIECES_X)),
            sem((2, max(2 * len(near + far), 1))),
            sem((2, max(n_tp - 1, 1))),
            sem((2, z_copies)),
            sem((2, PIECES_Z)),
            sem((2, PIECES_Z)),
            pltpu.SemaphoreType.REGULAR((2,)),
        ],
        compiler_params=pltpu.CompilerParams(collective_id=0, has_side_effects=True),
        name="step",
    )(
        hidden[0],
        down_weight,
        out_grad[0],
        pseudo_grad.reshape(n_x, 2, share, width),
        momentum,
    )
    lay, hg, nm, out = pl.pallas_call(
        store,
        out_shape=tuple(jax.ShapeDtypeStruct(r.shape, r.dtype) for r in results),
        in_specs=[vmem] * 4,
        out_specs=(any_ref,) * 4,
        scratch_shapes=[sem((4,))],
        compiler_params=pltpu.CompilerParams(vmem_limit_bytes=1 << 20),
        name="store",
    )(*results)
    return lay[None], hg[None], nm, out.reshape(down_weight.shape)


def solution(mesh):
    sizes = tuple(mesh.shape[axis] for axis in ("rep", "dp", "tp"))
    return jax.shard_map(
        functools.partial(per_device, sizes),
        mesh=mesh,
        in_specs=(
            P("rep", None, "tp"),
            P("tp", "dp"),
            P("rep", "tp", "dp"),
            P("rep", "tp", "dp"),
            P(("tp", "rep"), "dp"),
        ),
        out_specs=(
            P("rep", "tp", "dp"),
            P("rep", "dp", "tp"),
            P(("tp", "rep"), "dp"),
            P("tp", "dp"),
        ),
        check_vma=False,
    )
```

time: 181 us -> 64.6 us (0.36)
  the two profiles are of different devices: /device:TPU:2 before, /device:TPU:15 now
where the time goes in v2:
time: 64.6 us; the launch traced here: 64.1 us
  Pallas kernels  63.5 us (98%)
    pallas_call x1, Pallas kernels, per_device(): pl.pallas_call(functools.partial(kernel, n_rep, n_dp, n_tp), out_shape=(p...  62 us
    pallas_call x1, Pallas kernels, per_device(): pl.pallas_call(store, out_shape=tuple((jax.ShapeDtypeStruct(r.shape, r.dt...  1.48 us

profile of v2, /device:TPU:15, one launch (start us, length us, event | category | flops | bytes accessed | tf_op | source)
XLA Modules:
  0.0 64.1 jit_solution(8591087982711818551)
XLA Ops:
  0.6 62.0 %step.1 = (bf16[64,512]{1,0:T(8,128)(2,1)S(1)}, bf16[32,1792]{1,0:T(8,128)(2,1)S(1)}, f32[224,512]{1,0:T(8,128)S(1)}, bf16[4,2,224,512]{3,2,1,0:T(8,128)(2,1)S(1)}) custom-call(bf16[512,1792]{1,0:T(8,128)(2,1)} %bitcast.6, bf16[1792,512]{1,0:T(8,128)(2,1)} %w.1, bf16[64,512]{1,0:T(8,128)(2,1)} %bitcast.8, bf16[4,2,224,512]{3,2,1,0:T(8,128)(2,1)} %bitcast.7, ...), custom_call_target="tpu_custom_call" | custom-call | tf_op jit(solution)/shard_map/step/pallas_call | solution.py:413
  62.6 1.5 %store.1 = (bf16[64,512]{1,0:T(8,128)(2,1)}, bf16[32,1792]{1,0:T(8,128)(2,1)}, f32[224,512]{1,0:T(8,128)}, bf16[4,2,224,512]{3,2,1,0:T(8,128)(2,1)}) custom-call(bf16[64,512]{1,0:T(8,128)(2,1)S(1)} %get-tuple-element.12.refs_0_, bf16[32,1792]{1,0:T(8,128)(2,1)S(1)} %get-tuple-element.13.refs_1_, f32[224,512]{1,0:T(8,128)S(1)} %get-tuple-element.14.refs_2_, ...), custom_call_target="tpu_custom_call" | custom-call | tf_op jit(solution)/shard_map/store/pallas_call | solution.py:463

commit v3 on v2

--- a/solution.py
+++ b/solution.py
@@ -88,7 +88,7 @@
         for where in peers:
             pl.semaphore_signal(barrier, inc=1, device_id=where, device_id_type=MESH)
 
-    MOM, OG, HID, NM, LAY = range(n_x, n_x + 5)
+    MOM, OG, HID, NM, LAY = range(n_x * PIECES_X, n_x * PIECES_X + 5)
 
     def x_program():
         sent, loads = [], {}
@@ -114,10 +114,12 @@
         index = {key: i for i, key in enumerate(ring_items(n_x, PIECES_X))}
         rs, ag, ready = {}, {}, set()
 
-        def have(k):
+        def have(k, c):
+            if (k, c) not in ready:
+                ready.add((k, c))
+                arrived(dd.at[k, :, :, span(width, PIECES_X, c)], give_sem, k * PIECES_X + c)
             if k not in ready:
                 ready.add(k)
-                arrived(dd.at[k], give_sem, k)
                 loads[k].wait()
 
         def rs_send(s, h, d, c):
@@ -146,7 +148,7 @@
             hand_out((-s * d) % n_x, h, c)
 
         def rs_end(c):
-            have(0)
+            have(0, c)
             cols = span(width, PIECES_X, c)
             for h in (0, 1):
                 total = pgm[0, h, :, cols].astype(F32) + dd[0, h, :, cols].astype(F32)
@@ -177,7 +179,7 @@
             if arm(n_x, s, h) >= 1
         )
         for c, d, s, h in starts:
-            have((s * -d) % n_x)
+            have((s * -d) % n_x, c)
             rs_send(s, h, -d, c)
         for c in range(PIECES_X):
             for d in range(n_x // 2 - 1, 0, -1):
@@ -253,110 +255,143 @@
                 ref = ref.at[pl.ds(rows * half_rows, half_rows)]
             gathers[o, r] = go(remote(ref, ref, g_sem, g_index[o, r], to_y(o - relay)))
 
+        tile, f_tile = min(512, width), min(256, units)
+
+        def forward(r):
+            @pl.loop(0, width // tile)
+            def _(j):
+                cols = pl.ds(pl.multiple_of(j * tile, tile), tile)
+                block = jnp.dot(hid_v[r], w_v[:, cols], preferred_element_type=F32)
+                po[:, r, :, cols] = block.astype(BF16).reshape(n_y, -1, tile)
+
+        def gathered(r):
+            for key in gathers:
+                if key[1] == r and key not in relayed:
+                    gathers[key].wait_recv()
+
         loads["og"].wait()
         for item in near:
             gather(*item, 1)
-        for k in order_x:
-            go(remote(pg.at[at_x(k)], dd.at[k], give_sem, k, partner))
+        for c in range(PIECES_X):
+            for k in order_x:
+                cols = span(width, PIECES_X, c)
+                target = dd.at[k, :, :, cols]
+                go(remote(pg.at[at_x(k), :, :, cols], target, give_sem, k * PIECES_X + c, partner))
         go(remote(mom, mom_v.at[1], give_sem, MOM, partner))
+        loads["w"].wait()
+        loads["hid"].wait()
+        forward(1)
+        for item in far:
+            gather(*item, 1)
         arrived(og_v.at[0, slot_me], give_sem, OG)
         for item in near:
             gather(*item, 0)
-
-        loads["w"].wait()
-        f_tile = min(256, units)
 
         @pl.loop(0, units // f_tile)
         def _(j):
             cols = pl.ds(pl.multiple_of(j * f_tile, f_tile), f_tile)
             wt_v[:, cols] = w_v[cols, :].T
 
-        for r in (1, 0):
-            for item in far:
-                gather(*item, r)
-
-        loads["hid"].wait()
+        def back(a, b, r):
+            wide = units // 2
+
+            @pl.loop(0, 2)
+            def _(j):
+                cols = pl.ds(pl.multiple_of(j * wide, wide), wide)
+                rows = og_v[r, pl.ds(a, b - a)].reshape(-1, width)
+                block = jnp.dot(rows, wt_v[:, cols], preferred_element_type=F32).astype(BF16)
+                part[pl.ds(a, b - a), :, r, :, cols] = block.reshape(b - a, 2, -1, wide)
+
+        z_index = {key: i for i, key in enumerate(ring_items(n_z, 2 * PIECES_Z))}
+        zs = {}
+
+        def z_slot(k):
+            return (k - shift) % n_z
+
+        def z_send(s, h, d, r, c):
+            k = z_slot(s * d)
+            cols = span(units, PIECES_Z, c)
+            i = r * PIECES_Z + c
+            if d < arm(n_z, s, h):
+                zs[s, h, d + 1, i].wait_recv()
+                total = part[k, h, r, :, cols].astype(F32) + brecv[sign_at(s), h, d, r, :, cols].astype(F32)
+                part[k, h, r, :, cols] = total.astype(BF16)
+            target = brecv.at[sign_at(s), h, d - 1, r, :, cols]
+            zs[s, h, d, i] = go(remote(part.at[k, h, r, :, cols], target, b_sem, z_index[s, h, d, i], to_z(s)))
+
+        def z_wave(step, r):
+            for long_arm in (True, False):
+                for c in range(PIECES_Z):
+                    for s in (1, -1):
+                        h = 0 if (s > 0) == long_arm else 1
+                        d = arm(n_z, s, h) - step
+                        if d >= 1:
+                            z_send(s, h, d, r, c)
+
+        ends = {}
+
+        def z_end(r):
+            for c in range(PIECES_Z):
+                i = r * PIECES_Z + c
+                cols = span(units, PIECES_Z, c)
+                for h in (0, 1):
+                    total = part[z_slot(0), h, r, :, cols].astype(F32)
+                    for s in (1, -1):
+                        if arm(n_z, s, h) >= 1:
+                            zs[s, h, 1, i].wait_recv()
+                            total = total + brecv[sign_at(s), h, 0, r, :, cols].astype(F32)
+                    fin[h, r, :, cols] = total
+                xs[r, :, cols] = fin[1 - low, r, :, cols].astype(BF16)
+                ends[i] = go(remote(xs.at[r, :, cols], xrv.at[r, :, cols], e_sem, i, pair))
+
+        def grad_out(r):
+            for c in range(PIECES_Z):
+                i = r * PIECES_Z + c
+                cols = span(units, PIECES_Z, c)
+                ends[i].wait_recv()
+                total = (fin[low, r, :, cols] + xrv[r, :, cols].astype(F32)).astype(BF16)
+                if r == 1:
+                    hg_o[:, cols] = total
+                else:
+                    hg_v[:, cols] = total
+                    go(remote(hg_v.at[:, cols], hg_o.at[:, cols], h_sem, c, partner))
+
+        cut = min(3, n_z)
+        last = n_z // 2 - 1
+        gathered(1)
+        back(0, cut, 1)
+        if n_z > 1:
+            for s in (1, -1):
+
+                @pl.when(lower_than[s])
+                def _():
+                    pl.semaphore_wait(z_sem.at[sign_at(s)], 1)
+
+        z_wave(0, 1)
+        for item in far:
+            gather(*item, 0)
+        if cut < n_z:
+            back(cut, n_z, 1)
         arrived(hid_v.at[0], give_sem, HID)
-        tile = min(256, width)
-
-        @pl.loop(0, width // tile)
-        def _(j):
-            cols = pl.ds(pl.multiple_of(j * tile, tile), tile)
-            for r in (0, 1):
-                block = jnp.dot(hid_v[r], w_v[:, cols], preferred_element_type=F32)
-                po[:, r, :, cols] = block.astype(BF16).reshape(n_y, -1, tile)
-
-        for key in gathers:
-            if key not in relayed:
-                gathers[key].wait_recv()
-
+        if last >= 1:
+            z_wave(1, 1)
+        gathered(0)
+        back(0, cut, 0)
+        z_wave(0, 0)
+        forward(0)
         exchange = {}
         for o in range(1, n_y):
             exchange[o] = go(remote(po.at[lax.rem(y + o, n_y)], lrecv.at[o - 1], l_sem, o - 1, to_y(o)))
-
-        def back(a, b):
-            @pl.loop(0, units // f_tile)
-            def _(j):
-                cols = pl.ds(pl.multiple_of(j * f_tile, f_tile), f_tile)
-                rows = og_v[:, pl.ds(a, b - a)].reshape(-1, width)
-                block = jnp.dot(rows, wt_v[:, cols], preferred_element_type=F32).astype(BF16)
-                block = block.reshape(2, b - a, 2, -1, f_tile)
-                for r in (0, 1):
-                    part[pl.ds(a, b - a), :, r, :, cols] = block[r]
-
-        z_index = {key: i for i, key in enumerate(ring_items(n_z, PIECES_Z))}
-        zs = {}
-
-        def z_slot(k):
-            return (k - shift) % n_z
-
-        def z_send(s, h, d, c):
-            k = z_slot(s * d)
-            cols = span(units, PIECES_Z, c)
-            if d < arm(n_z, s, h):
-                zs[s, h, d + 1, c].wait_recv()
-                total = part[k, h, :, :, cols].astype(F32) + brecv[sign_at(s), h, d, :, :, cols].astype(F32)
-                part[k, h, :, :, cols] = total.astype(BF16)
-            target = brecv.at[sign_at(s), h, d - 1, :, :, cols]
-            zs[s, h, d, c] = go(remote(part.at[k, h, :, :, cols], target, b_sem, z_index[s, h, d, c], to_z(s)))
-
-        def z_wave(step, long_arm):
-            for c in range(PIECES_Z):
-                for s in (1, -1):
-                    h = 0 if (s > 0) == long_arm else 1
-                    d = arm(n_z, s, h) - step
-                    if d >= 1:
-                        z_send(s, h, d, c)
-
-        cut = min(3, n_z)
-        back(0, cut)
-        if n_z > 1:
-            for s in (1, -1):
-
-                @pl.when(lower_than[s])
-                def _():
-                    pl.semaphore_wait(z_sem.at[sign_at(s)], 1)
-
-        z_wave(0, True)
-        z_wave(0, False)
         if cut < n_z:
-            back(cut, n_z)
-        for step in range(1, n_z // 2):
-            z_wave(step, True)
-            z_wave(step, False)
-
-        ends = {}
-        for c in range(PIECES_Z):
-            cols = span(units, PIECES_Z, c)
-            for h in (0, 1):
-                total = part[z_slot(0), h, :, :, cols].astype(F32)
-                for s in (1, -1):
-                    if arm(n_z, s, h) >= 1:
-                        zs[s, h, 1, c].wait_recv()
-                        total = total + brecv[sign_at(s), h, 0, :, :, cols].astype(F32)
-                fin[h, :, :, cols] = total
-            xs[:, :, cols] = fin[1 - low, :, :, cols].astype(BF16)
-            ends[c] = go(remote(xs.at[:, :, cols], xrv.at[:, :, cols], e_sem, c, pair))
+            back(cut, n_z, 0)
+        for step in range(2, last + 1):
+            z_wave(step, 1)
+            z_wave(step - 1, 0)
+        z_end(1)
+        if last >= 1:
+            z_wave(last, 0)
+        z_end(0)
+        grad_out(1)
 
         total = po[y].astype(F32)
         for o in range(1, n_y):
@@ -365,14 +400,7 @@
         lay_v[...] = total[0].astype(BF16)
         lay_o[...] = total[1].astype(BF16)
         go(remote(lay_v, lay_o, give_sem, LAY, partner))
-
-        for c in range(PIECES_Z):
-            cols = span(units, PIECES_Z, c)
-            ends[c].wait_recv()
-            total = fin[low, :, :, cols] + xrv[:, :, cols].astype(F32)
-            hg_v[:, cols] = total[0].astype(BF16)
-            hg_o[:, cols] = total[1].astype(BF16)
-            go(remote(hg_v.at[:, cols], hg_o.at[:, cols], h_sem, c, partner))
+        grad_out(0)
 
         for k in range(n_x):
             for h in (0, 1):
@@ -405,7 +433,7 @@
     owned = tokens // n_dp
     far_x, far_z = max(n_x // 2, 1), max(n_z // 2, 1)
     x_copies = max(len(ring_items(n_x, PIECES_X)), 1)
-    z_copies = max(len(ring_items(n_z, PIECES_Z)), 1)
+    z_copies = max(len(ring_items(n_z, 2 * PIECES_Z)), 1)
     near, far = gather_plan(n_tp)
     any_ref = pl.BlockSpec(memory_space=pl.ANY)
     vmem = pl.BlockSpec(memory_space=pltpu.VMEM)
@@ -440,14 +468,14 @@
             pltpu.VMEM((2, owned, units), BF16),
             pltpu.VMEM((owned, units), BF16),
             sem((max(n_x + 1, 3),)),
-            sem((2, n_x + 5)),
+            sem((2, n_x * PIECES_X + 5)),
             sem((2, x_copies)),
             sem((2, x_copies)),
             sem((2, 2 * n_x * PIECES_X)),
             sem((2, max(2 * len(near + far), 1))),
             sem((2, max(n_tp - 1, 1))),
             sem((2, z_copies)),
-            sem((2, PIECES_Z)),
+            sem((2, 2 * PIECES_Z)),
             sem((2, PIECES_Z)),
             pltpu.SemaphoreType.REGULAR((2,)),
         ],

time: 64.6 us -> 61.6 us (0.954)
  Pallas kernels: 63.5 us -> 60.8 us
    pallas_call x1, Pallas kernels: 62 us -> 59.3 us  [per_device(): pl.pallas_call(functools.partial(kernel, n_rep, n_dp, n_tp), out_shape=(p...]
where the time goes in v3:
time: 61.6 us; the launch traced here: 61.5 us
  Pallas kernels  60.8 us (99%)
  between operations  0.64 us (1%)
    pallas_call x1, Pallas kernels, per_device(): pl.pallas_call(functools.partial(kernel, n_rep, n_dp, n_tp), out_shape=(p...  59.3 us
    pallas_call x1, Pallas kernels, per_device(): pl.pallas_call(store, out_shape=tuple((jax.ShapeDtypeStruct(r.shape, r.dt...  1.48 us

profile of v3, /device:TPU:15, one launch (start us, length us, event | category | flops | bytes accessed | tf_op | source)
XLA Modules:
  0.0 61.5 jit_solution(894162530455053815)
XLA Ops:
  0.6 59.3 %step.1 = (bf16[64,512]{1,0:T(8,128)(2,1)S(1)}, bf16[32,1792]{1,0:T(8,128)(2,1)S(1)}, f32[224,512]{1,0:T(8,128)S(1)}, bf16[4,2,224,512]{3,2,1,0:T(8,128)(2,1)S(1)}) custom-call(bf16[512,1792]{1,0:T(8,128)(2,1)} %bitcast.6, bf16[1792,512]{1,0:T(8,128)(2,1)} %w.1, bf16[64,512]{1,0:T(8,128)(2,1)} %bitcast.8, bf16[4,2,224,512]{3,2,1,0:T(8,128)(2,1)} %bitcast.7, ...), custom_call_target="tpu_custom_call" | custom-call | tf_op jit(solution)/shard_map/step/pallas_call | solution.py:441
  60.0 1.5 %store.1 = (bf16[64,512]{1,0:T(8,128)(2,1)}, bf16[32,1792]{1,0:T(8,128)(2,1)}, f32[224,512]{1,0:T(8,128)}, bf16[4,2,224,512]{3,2,1,0:T(8,128)(2,1)}) custom-call(bf16[64,512]{1,0:T(8,128)(2,1)S(1)} %get-tuple-element.12.refs_0_, bf16[32,1792]{1,0:T(8,128)(2,1)S(1)} %get-tuple-element.13.refs_1_, f32[224,512]{1,0:T(8,128)S(1)} %get-tuple-element.14.refs_2_, ...), custom_call_target="tpu_custom_call" | custom-call | tf_op jit(solution)/shard_map/store/pallas_call | solution.py:491

commit v4 on v3

--- a/solution.py
+++ b/solution.py
@@ -194,8 +194,9 @@
         go(remote(nm_v, nm_o, give_sem, NM, partner))
         for d in range(1, n_x // 2 + 1):
             for c in range(PIECES_X):
-                for s in (1, -1):
-                    for h in (0, 1):
+                for far_first in (True, False):
+                    for s in (1, -1):
+                        h = 0 if (s > 0) == far_first else 1
                         if d <= arm(n_x, s, h):
                             ag_take(s, h, d, c)
         arrived(lay_o, give_sem, LAY)
@@ -392,6 +393,7 @@
             z_wave(last, 0)
         z_end(0)
         grad_out(1)
+        grad_out(0)
 
         total = po[y].astype(F32)
         for o in range(1, n_y):
@@ -400,7 +402,6 @@
         lay_v[...] = total[0].astype(BF16)
         lay_o[...] = total[1].astype(BF16)
         go(remote(lay_v, lay_o, give_sem, LAY, partner))
-        grad_out(0)
 
         for k in range(n_x):
             for h in (0, 1):

time: 61.6 us -> 61.8 us (level)
  no operation moved by 1% of the time
where the time goes in v4:
time: 61.8 us; the launch traced here: 61.7 us
  Pallas kernels  61 us (99%)
  between operations  0.64 us (1%)
    pallas_call x1, Pallas kernels, per_device(): pl.pallas_call(functools.partial(kernel, n_rep, n_dp, n_tp), out_shape=(p...  59.6 us
    pallas_call x1, Pallas kernels, per_device(): pl.pallas_call(store, out_shape=tuple((jax.ShapeDtypeStruct(r.shape, r.dt...  1.48 us

profile of v4, /device:TPU:15, one launch (start us, length us, event | category | flops | bytes accessed | tf_op | source)
XLA Modules:
  0.0 61.7 jit_solution(6200194435803507299)
XLA Ops:
  0.6 59.6 %step.1 = (bf16[64,512]{1,0:T(8,128)(2,1)S(1)}, bf16[32,1792]{1,0:T(8,128)(2,1)S(1)}, f32[224,512]{1,0:T(8,128)S(1)}, bf16[4,2,224,512]{3,2,1,0:T(8,128)(2,1)S(1)}) custom-call(bf16[512,1792]{1,0:T(8,128)(2,1)} %bitcast.6, bf16[1792,512]{1,0:T(8,128)(2,1)} %w.1, bf16[64,512]{1,0:T(8,128)(2,1)} %bitcast.8, bf16[4,2,224,512]{3,2,1,0:T(8,128)(2,1)} %bitcast.7, ...), custom_call_target="tpu_custom_call" | custom-call | tf_op jit(solution)/shard_map/step/pallas_call | solution.py:442
  60.2 1.5 %store.1 = (bf16[64,512]{1,0:T(8,128)(2,1)}, bf16[32,1792]{1,0:T(8,128)(2,1)}, f32[224,512]{1,0:T(8,128)}, bf16[4,2,224,512]{3,2,1,0:T(8,128)(2,1)}) custom-call(bf16[64,512]{1,0:T(8,128)(2,1)S(1)} %get-tuple-element.12.refs_0_, bf16[32,1792]{1,0:T(8,128)(2,1)S(1)} %get-tuple-element.13.refs_1_, f32[224,512]{1,0:T(8,128)S(1)} %get-tuple-element.14.refs_2_, ...), custom_call_target="tpu_custom_call" | custom-call | tf_op jit(solution)/shard_map/store/pallas_call | solution.py:492
